TPU v7x, 256 devices: a whole 4x4x8 slice. The times are simulated.
256 devices in a mesh: dap: 16 (over x, z_lo), cplx: 16 (over y, z_hi, core).
Axes of the slice: x: 4, y: 4, z: 8 (z_hi: 2, z_lo: 4; z = z_hi * 4 + z_lo), core: 2. Of those that a mesh axis runs over, the one named last changes fastest.
Arguments:
- pair: bfloat16 [192, 3072, 128], P('dap', 'cplx'), parts along dimension 1, may hold values from -6 to 6
- cotangent: bfloat16 [192, 3072, 128], P('dap', 'cplx'), parts along dimension 1, may hold values from -6 to 6
- residue_mask: int32 [3072], P('cplx'), parts along dimension 0, may hold values 0 or 1
- chain_ids: int32 [3072], P('cplx'), parts along dimension 0, may hold values from 0 to 2, never falling along the last dimension, each value on 1 to 96 neighbouring positions
- chain_embed: float32 [2, 128], replicated, may hold values from -4 to 4
- out_norm_gain: float32 [128], replicated, may hold values from 0.25 to 1.75
- out_proj: bfloat16 [128, 512], replicated, may hold values from -0.5 to 0.5
- out_gate: bfloat16 [128, 128], replicated, may hold values from -0.5 to 0.5
- out_mid_gain: float32 [128], replicated, may hold values from 0.25 to 1.75
- out_final: bfloat16 [128, 128], replicated, may hold values from -0.5 to 0.5
- in_norm_gain: float32 [128], replicated, may hold values from 0.25 to 1.75
- in_proj: bfloat16 [128, 512], replicated, may hold values from -0.5 to 0.5
- in_gate: bfloat16 [128, 128], replicated, may hold values from -0.5 to 0.5
- in_mid_gain: float32 [128], replicated, may hold values from 0.25 to 1.75
- in_final: bfloat16 [128, 128], replicated, may hold values from -0.5 to 0.5
Outputs:
- pair_grad: bfloat16 [192, 3072, 128], P('dap', 'cplx'), parts along dimension 1
- grad_proj: float32 [2048, 512], P('cplx'), parts along dimension 0
- grad_gate: float32 [2048, 128], P('cplx'), parts along dimension 0
- grad_final: float32 [2048, 128], P('cplx'), parts along dimension 0
- grad_norm_gain: float32 [2048], P('cplx'), parts along dimension 0
- grad_mid_gain: float32 [2048], P('cplx'), parts along dimension 0
There are 16 independent parts, one for each index of `cplx`. A program takes and returns all parts, laid end to end along the dimension named above; an argument that names none is the same for every part. Nothing has to cross between parts.
Inputs may be any that keep to these rules, and one draw needn't show every extreme that they name: `chain_ids`: chain numbers never fall along the residues; each chain has at most 96 residues.
All inputs are finite; a program needn't handle non-finite values.
Results may differ from a plain program's by a relative error of at most 0.019.
Values may be sent and summed in bfloat16 or wider, within the bound.
No kernel may reach another device: no remote copies, remote signals or barrier semaphores. Data moves between devices by JAX's collectives and lax.ppermute only.
A program may use at most 128 MiB of HBM per device.

v0:
```python
import jax
import jax.numpy as jnp
from jax import lax
from jax.sharding import PartitionSpec as P


def together(arrays, axis):
    ends = [0]
    for a in arrays:
        ends.append(ends[-1] + a.size)
    subtotal = lax.psum(jnp.concatenate([a.ravel() for a in arrays]), axis)
    return tuple((subtotal[b:e].reshape(a.shape) for a, b, e in zip(arrays, ends, ends[1:])))


def layer_norm(values_in, gain):
    average = jnp.mean(values_in, axis=-1, keepdims=True)
    centred = values_in - average
    variance = jnp.mean(centred * centred, axis=-1, keepdims=True)
    return centred * lax.rsqrt(variance + 1e-05) * gain


def gated_pair(projected, pair_mask, hidden_width):
    masked = pair_mask[..., None]
    left_act = (
        masked
        * jax.nn.sigmoid(projected[..., :hidden_width])
        * projected[..., hidden_width : 2 * hidden_width]
    )
    right_act = (
        masked
        * jax.nn.sigmoid(projected[..., 2 * hidden_width : 3 * hidden_width])
        * projected[..., 3 * hidden_width :]
    )
    return (left_act, right_act)


def shards(
    pair,
    cotangent,
    residue_mask,
    chain_ids,
    chain_embed,
    out_norm_gain,
    out_proj,
    out_gate,
    out_mid_gain,
    out_final,
    in_norm_gain,
    in_proj,
    in_gate,
    in_mid_gain,
    in_final,
):
    f32 = jnp.float32
    bf16 = jnp.bfloat16
    row_count = pair.shape[0]
    res_count = pair.shape[1]
    hidden_width = out_final.shape[0]
    inv_count = 1.0 / res_count
    row_start = lax.axis_index("dap") * row_count
    row_mask = lax.dynamic_slice_in_dim(residue_mask, row_start, row_count, 0)
    row_chain = lax.dynamic_slice_in_dim(chain_ids, row_start, row_count, 0)
    pair_mask = (row_mask[:, None] * residue_mask[None, :]).astype(f32)
    same_chain = row_chain[:, None] == chain_ids[None, :]
    start = pair.astype(f32) + jnp.where(same_chain[..., None], chain_embed[1], chain_embed[0])
    out_normed = layer_norm(start, out_norm_gain).astype(bf16)
    projected = jnp.dot(out_normed, out_proj, preferred_element_type=f32)
    left_act, right_act = gated_pair(projected, pair_mask, hidden_width)
    left_b = left_act.astype(bf16)
    right_b = right_act.astype(bf16)
    x_out = jnp.einsum(
        "ikc,jkc->ijc",
        left_b,
        lax.all_gather(right_b, "dap", axis=0, tiled=True),
        preferred_element_type=f32,
    )
    y_out = layer_norm(x_out, out_mid_gain).astype(bf16)
    update = jax.nn.sigmoid(jnp.dot(out_normed, out_gate, preferred_element_type=f32)) * jnp.dot(
        y_out, out_final, preferred_element_type=f32
    )
    pair_mid = (start + update).astype(bf16)
    mid_f32 = pair_mid.astype(f32)
    normed_f32, norm_back = jax.vjp(layer_norm, mid_f32, in_norm_gain)
    in_normed = normed_f32.astype(bf16)
    proj_in = jnp.dot(in_normed, in_proj, preferred_element_type=f32)
    (left_in, right_in), glu_back = jax.vjp(
        lambda proj_val: gated_pair(proj_val, pair_mask, hidden_width), proj_in
    )
    left_ib = left_in.astype(bf16)
    right_ib = right_in.astype(bf16)
    columns = lax.all_to_all(left_ib, "dap", split_axis=1, concat_axis=0, tiled=True)
    left_block = columns
    x_in = jnp.einsum(
        "kic,kjc->ijc",
        left_block,
        lax.all_gather(right_ib, "dap", axis=0, tiled=True),
        preferred_element_type=f32,
    )
    y_f32, mid_back = jax.vjp(layer_norm, x_in, in_mid_gain)
    y_in = y_f32.astype(bf16)
    logit = jnp.dot(in_normed, in_gate, preferred_element_type=f32)
    value = jnp.dot(y_in, in_final, preferred_element_type=f32)
    sigma = jax.nn.sigmoid(logit)
    upstream = cotangent.astype(f32)
    grad_value = (upstream * sigma).astype(bf16)
    grad_logit = (upstream * value * sigma * (1.0 - sigma)).astype(bf16)
    grad_final = jnp.einsum("ijc,ijd->cd", y_in, grad_value, preferred_element_type=f32) * inv_count
    grad_gate = (
        jnp.einsum("ijc,ijd->cd", in_normed, grad_logit, preferred_element_type=f32) * inv_count
    )
    grad_y = jnp.dot(grad_value, in_final.T, preferred_element_type=f32)
    grad_x, grad_mid = mid_back(grad_y)
    grad_x_b = grad_x.astype(bf16)
    shard_rows = lax.all_gather(grad_x_b, "dap", axis=0, tiled=True)
    left_block = left_ib
    grad_right = jnp.einsum("kic,ijc->kjc", left_block, shard_rows, preferred_element_type=f32)
    new_block = jnp.einsum("kjc,ijc->kic", right_ib, shard_rows, preferred_element_type=f32)
    grad_p = glu_back((new_block, grad_right))[0].astype(bf16)
    grad_proj = jnp.einsum("ijc,ijd->cd", in_normed, grad_p, preferred_element_type=f32) * inv_count
    grad_normed = jnp.dot(grad_p, in_proj.T, preferred_element_type=f32) + jnp.dot(
        grad_logit, in_gate.T, preferred_element_type=f32
    )
    grad_z, grad_norm = norm_back(grad_normed)
    pair_grad = (upstream + grad_z).astype(bf16)
    reduced = tuple(
        (
            part.astype(jnp.float32)
            for part in together(
                (
                    grad_proj.astype(jnp.bfloat16),
                    grad_gate.astype(jnp.bfloat16),
                    grad_final.astype(jnp.bfloat16),
                    (grad_norm * inv_count).astype(jnp.bfloat16),
                    (grad_mid * inv_count).astype(jnp.bfloat16),
                ),
                "dap",
            )
        )
    )
    return (pair_grad, reduced[0], reduced[1], reduced[2], reduced[3], reduced[4])


def solution(mesh):
    placed = (
        P("dap", "cplx", None),
        P("dap", "cplx", None),
        P("cplx"),
        P("cplx"),
        P(),
        P(),
        P(),
        P(),
        P(),
        P(),
        P(),
        P(),
        P(),
        P(),
        P(),
    )
    return jax.shard_map(
        shards,
        mesh=mesh,
        in_specs=placed,
        out_specs=(
            P("dap", "cplx", None),
            P("cplx", None),
            P("cplx", None),
            P("cplx", None),
            P("cplx"),
            P("cplx"),
        ),
        check_vma=False,
    )
```

profile of v0, /device:TPU:8, one launch (start us, length us, event | category | flops | bytes accessed | tf_op | source)
XLA Modules:
  0.0 931.0 jit_solution(3358620269729586650)
XLA Ops:
  7.3 0.8 dynamic_slice.7
  9.6 1.9 fusion.44
  11.6 2.3 multiply_reduce_fusion.4
  14.1 1.1 fusion.58
  15.2 1.5 fusion.31
  16.7 1.9 copy.47
  18.7 2.8 fusion.12
  21.5 204.8 %all-gather.4.cloned.1.call-done = bf16[192,192,128]{2,1,0:T(8,128)(2,1)} async-done(((bf16[12,192,128]{2,1,0:T(8,128)(2,1)}), bf16[192,192,128]{2,1,0:T(8,128)(2,1)}) %all-gather.4.cloned.1.call-update) | async-done | bytes 9437200 | tf_op jit(solution)/shard_map/all_gather | solution.py:74
  226.2 17.4 %copy.46 = bf16[192,192,128]{1,0,2:T(8,128)(2,1)} copy(bf16[192,192,128]{2,1,0:T(8,128)(2,1)} %all-gather.4.cloned.1.call-done) | data formatting | bytes 18874368 | tf_op jit(solution)/shard_map/all_gather | solution.py:74
  243.6 8.2 bitcast_reduce_fusion
  252.8 1.0 copy-done.8
  253.8 1.6 convert_reduce_fusion
  255.4 0.8 fusion.19
  256.2 0.8 fusion.62
  257.1 2.0 multiply_convert_fusion.2
  259.4 1.3 copy.49
  260.7 4.3 all-to-all-start
  266.1 41.9 %all-to-all-done = bf16[12,192,128]{2,0,1:T(8,128)(2,1)} async-done(((bf16[12,192,128]{2,0,1:T(8,128)(2,1)}), bf16[12,192,128]{2,0,1:T(8,128)(2,1)}, u32[]{:S(2)}, u32[]{:S(2)}) %all-to-all-start) | async-done | bytes 589856 | tf_op jit(solution)/shard_map/all_to_all | solution.py:91
  308.0 1.3 copy.51
  309.3 0.9 all_to_all.16
  310.2 1.8 copy.53
  312.1 163.0 %all-gather.6.cloned.1.call-done = bf16[192,192,128]{2,1,0:T(8,128)(2,1)} async-done(((bf16[12,192,128]{2,1,0:T(8,128)(2,1)}), bf16[192,192,128]{2,1,0:T(8,128)(2,1)}) %all-gather.6.cloned.1.call-update) | async-done | bytes 9437200 | tf_op jit(solution)/shard_map/all_gather | solution.py:96
  475.0 17.4 %copy.52 = bf16[192,192,128]{1,0,2:T(8,128)(2,1)} copy(bf16[192,192,128]{2,1,0:T(8,128)(2,1)} %all-gather.6.cloned.1.call-done) | data formatting | bytes 18874368 | tf_op jit(solution)/shard_map/all_gather | solution.py:96
  492.4 7.6 fusion.82
  500.1 2.2 copy.54
  503.4 1.3 multiply_reduce_fusion.3
  504.7 1.7 multiply_reduce_fusion.1
  506.4 2.3 add_convert_fusion.1
  509.1 2.6 copy.59
  511.7 2.6 copy.56
  514.3 2.7 fusion.15
  517.0 198.6 %all-gather.8.cloned.1.call-done = bf16[192,192,128]{2,1,0:T(8,128)(2,1)} async-done(((bf16[12,192,128]{2,1,0:T(8,128)(2,1)}), bf16[192,192,128]{2,1,0:T(8,128)(2,1)}) %all-gather.8.cloned.1.call-update) | async-done | bytes 9437200 | tf_op jit(solution)/shard_map/all_gather | solution.py:114
  715.6 17.4 %copy.55 = bf16[192,192,128]{1,0,2:T(8,128)(2,1)} copy(bf16[192,192,128]{2,1,0:T(8,128)(2,1)} %all-gather.8.cloned.1.call-done) | data formatting | bytes 18874368 | tf_op jit(solution)/shard_map/all_gather | solution.py:114
  733.0 9.5 %fusion.84 = f32[128,192,12]{1,2,0:T(8,128)} fusion(bf16[192,192,128]{1,0,2:T(8,128)(2,1)} %copy.55, bf16[12,192,128]{1,0,2:T(8,128)(2,1)} %copy.59), kind=kOutput, calls=%fused_computation.145 | convolution fusion | flops 113246208 | bytes 11206656 | tf_op jit(solution)/shard_map/kjc,ijc->kic/dot_general | solution.py:117
  742.5 2.7 copy.60
  745.2 7.9 fusion.83
  753.1 2.7 copy.57
  755.8 3.7 bitcast_multiply_fusion.3
  759.5 1.2 fusion.47
  761.8 1.0 fusion.52
  762.9 1.1 fusion.55
  763.9 0.8 fusion.20
  764.8 1.7 fusion.18
  767.7 2.5 fusion.22
  770.2 149.9 %all-reduce.6.cloned.1.call-done = bf16[98560]{0:T(1024)(128)(2,1)} async-done(((bf16[98560]{0:T(1024)(128)(2,1)}), bf16[98560]{0:T(1024)(128)(2,1)}) %all-reduce.6.cloned.1.call-update) | async-done | bytes 197136 | tf_op jit(solution)/shard_map/psum | solution.py:11
  920.1 0.9 slice_convert_fusion
  921.8 1.4 fusion.65
  923.2 1.3 slice_convert_fusion.1
  (74 shorter events, 8.4 us)
Async XLA Ops:
  7.2 249.1 %copy-start = (bf16[128,512]{1,0:T(8,128)(2,1)S(1)}, bf16[128,512]{1,0:T(8,128)(2,1)}, u32[]{:S(2)}) copy-start(bf16[128,512]{1,0:T(8,128)(2,1)} %param.26) | copy-start | bytes 393220
  7.2 6.9 copy-start.5
  7.2 6.7 copy-start.16
  7.2 6.8 copy-start.18
  7.2 6.8 copy-start.11
  7.2 219.0 %all-gather.4.cloned.1.call-start = ((), (), s32[]{:S(2)}) async-start(), calls=%async_computation.1 | async-start | bytes 10027008 | tf_op jit(solution)/shard_map/all_gather | solution.py:74
  16.7 2.0 copy-start.19
  16.7 458.3 %all-gather.6.cloned.1.call-start = ((), (), s32[]{:S(2)}) async-start(), calls=%async_computation.2 | async-start | bytes 10027008 | tf_op jit(solution)/shard_map/all_gather | solution.py:96
  251.8 0.7 copy-start.17
  252.5 1.3 copy-start.8
  252.5 1.3 copy-start.12
  253.8 2.5 copy-start.15
  257.1 2.3 copy-start.1
  259.4 1.3 copy-start.6
  259.4 5.8 copy-start.13
  260.7 47.2 %all-to-all-start = ((bf16[12,192,128]{2,0,1:T(8,128)(2,1)}), bf16[12,192,128]{2,0,1:T(8,128)(2,1)}, u32[]{:S(2)}, u32[]{:S(2)}) async-start(bf16[12,192,128]{2,0,1:T(8,128)(2,1)} %copy.49), calls=%async_computation | async-start | bytes 1572864 | tf_op jit(solution)/shard_map/all_to_all | solution.py:91
  265.0 450.6 %all-gather.8.cloned.1.call-start = ((), (), s32[]{:S(2)}) async-start(), calls=%async_computation.3 | async-start | bytes 10027008 | tf_op jit(solution)/shard_map/all_gather | solution.py:114
  502.3 1.1 copy-start.2
  502.3 1.1 copy-start.10
  502.3 1.0 copy-start.14
  508.8 411.3 %all-reduce.6.cloned.1.call-start = ((), (), s32[]{:S(2)}) async-start(), calls=%async_computation.4 | async-start | bytes 397312 | tf_op jit(solution)/shard_map/psum | solution.py:11
  760.8 1.1 copy-start.7
  761.6 1.2 copy-start.3
  764.8 2.9 copy-start.4
  767.0 0.7 copy-start.9
Sparse Core Ops, SparseCore 0:
  16.8 209.3 all-gather.3
  259.5 215.4 all-gather.5
  508.9 206.6 all-gather.7
  767.8 152.2 all-reduce.5
where the time goes:
time: 933 us; the launch traced here: 931 us
  waiting for transfers between devices  758 us (81%)
  local copies, waits for them, and re-layouts  78.5 us (8%)
  matrix products  49.2 us (5%)
  other arithmetic  26.1 us (3%)
  between operations  14.2 us (2%)
    all_gather x1, waiting for transfers between devices, shards(): lax.all_gather(right_b, 'dap', axis=0, tiled=True)  205 us
    all_gather x1, waiting for transfers between devices, shards(): shard_rows = lax.all_gather(grad_x_b, 'dap', axis=0, tiled=True)  199 us
    all_gather x1, waiting for transfers between devices, shards(): lax.all_gather(right_ib, 'dap', axis=0, tiled=True)  163 us
    psum x1, waiting for transfers between devices, together(): subtotal = lax.psum(jnp.concatenate([a.ravel() for a in arrays]), axis)  150 us
    all_to_all x1, waiting for transfers between devices, shards(): lax.all_to_all(left_ib, 'dap', split_axis=1, concat_axis=0, tiled=True)  41.9 us
  transfers between devices with their start and end apart: 5, of which 5 were waited for; matrix products, arithmetic and copies ran while one was open for 2% of the time, Pallas kernels for 0%

commit v1 on v0

--- a/solution.py
+++ b/solution.py
@@ -8,7 +8,7 @@
     ends = [0]
     for a in arrays:
         ends.append(ends[-1] + a.size)
-    subtotal = lax.psum(jnp.concatenate([a.ravel() for a in arrays]), axis)
+    subtotal = jnp.sum(lax.all_gather(jnp.concatenate([a.ravel() for a in arrays]), axis), axis=0)
     return tuple((subtotal[b:e].reshape(a.shape) for a, b, e in zip(arrays, ends, ends[1:])))
 
 

time: 933 us -> 938 us (level)
  other arithmetic: 26.1 us -> 41.1 us
  waiting for transfers between devices: 758 us -> 748 us
    psum x1 -> x0, waiting for transfers between devices: 150 us -> none  [together(): subtotal = lax.psum(jnp.concatenate([a.ravel() for a in arrays]), axis)]
    all_gather x0 -> x1, waiting for transfers between devices: none -> 140 us  [together(): lax.all_gather(jnp.concatenate([a.ravel() for a in arrays]), axis)]
    reduce_sum x0 -> x1, other arithmetic: none -> 17.4 us  [together(): jnp.sum(lax.all_gather(jnp.concatenate([a.ravel() for a in arrays]), axis...]
where the time goes in v1:
time: 938 us; the launch traced here: 936 us
  waiting for transfers between devices  748 us (80%)
  local copies, waits for them, and re-layouts  78.8 us (8%)
  matrix products  49.3 us (5%)
  other arithmetic  41.1 us (4%)
  between operations  14.2 us (2%)
    all_gather x1, waiting for transfers between devices, shards(): lax.all_gather(right_b, 'dap', axis=0, tiled=True)  205 us
    all_gather x1, waiting for transfers between devices, shards(): shard_rows = lax.all_gather(grad_x_b, 'dap', axis=0, tiled=True)  199 us
    all_gather x1, waiting for transfers between devices, shards(): lax.all_gather(right_ib, 'dap', axis=0, tiled=True)  163 us
    all_gather x1, waiting for transfers between devices, together(): lax.all_gather(jnp.concatenate([a.ravel() for a in arrays]), axis)  140 us
    all_to_all x1, waiting for transfers between devices, shards(): lax.all_to_all(left_ib, 'dap', split_axis=1, concat_axis=0, tiled=True)  41.9 us
  transfers between devices with their start and end apart: 5, of which 5 were waited for; matrix products, arithmetic and copies ran while one was open for 2% of the time, Pallas kernels for 0%

profile of v1, /device:TPU:8, one launch (start us, length us, event | category | flops | bytes accessed | tf_op | source)
XLA Modules:
  0.0 936.1 jit_solution(15914234314161798681)
XLA Ops:
  7.3 0.8 dynamic_slice.7
  9.6 1.9 fusion.44
  11.6 2.3 multiply_reduce_fusion.4
  14.1 1.1 fusion.58
  15.2 1.5 fusion.31
  16.7 2.0 copy.47
  18.7 2.8 fusion.12
  21.5 204.7 %all-gather.7.cloned.1.call-done = bf16[192,192,128]{2,1,0:T(8,128)(2,1)} async-done(((bf16[12,192,128]{2,1,0:T(8,128)(2,1)}), bf16[192,192,128]{2,1,0:T(8,128)(2,1)}) %all-gather.7.cloned.1.call-update) | async-done | bytes 9437200 | tf_op jit(solution)/shard_map/all_gather | solution.py:74
  226.2 17.4 %copy.46 = bf16[192,192,128]{1,0,2:T(8,128)(2,1)} copy(bf16[192,192,128]{2,1,0:T(8,128)(2,1)} %all-gather.7.cloned.1.call-done) | data formatting | bytes 18874368 | tf_op jit(solution)/shard_map/all_gather | solution.py:74
  243.7 8.2 bitcast_reduce_fusion
  252.8 1.0 copy-done.8
  253.8 1.6 convert_reduce_fusion
  255.4 0.8 fusion.19
  256.2 0.8 fusion.62
  257.1 2.0 multiply_convert_fusion.2
  259.4 1.3 copy.49
  260.7 4.3 all-to-all-start
  265.3 0.8 fusion.9
  266.1 41.9 %all-to-all-done = bf16[12,192,128]{2,0,1:T(8,128)(2,1)} async-done(((bf16[12,192,128]{2,0,1:T(8,128)(2,1)}), bf16[12,192,128]{2,0,1:T(8,128)(2,1)}, u32[]{:S(2)}, u32[]{:S(2)}) %all-to-all-start) | async-done | bytes 589856 | tf_op jit(solution)/shard_map/all_to_all | solution.py:91
  308.0 1.3 copy.51
  309.3 0.9 all_to_all.16
  310.2 1.8 copy.53
  312.0 163.0 %all-gather.9.cloned.1.call-done = bf16[192,192,128]{2,1,0:T(8,128)(2,1)} async-done(((bf16[12,192,128]{2,1,0:T(8,128)(2,1)}), bf16[192,192,128]{2,1,0:T(8,128)(2,1)}) %all-gather.9.cloned.1.call-update) | async-done | bytes 9437200 | tf_op jit(solution)/shard_map/all_gather | solution.py:96
  475.0 17.4 %copy.52 = bf16[192,192,128]{1,0,2:T(8,128)(2,1)} copy(bf16[192,192,128]{2,1,0:T(8,128)(2,1)} %all-gather.9.cloned.1.call-done) | data formatting | bytes 18874368 | tf_op jit(solution)/shard_map/all_gather | solution.py:96
  492.4 7.7 fusion.82
  500.1 2.2 copy.54
  503.4 1.3 multiply_reduce_fusion.3
  504.7 1.7 multiply_reduce_fusion.1
  506.4 2.3 add_convert_fusion.1
  509.0 2.6 copy.59
  511.7 2.6 copy.56
  514.3 2.7 fusion.15
  517.0 198.6 %all-gather.11.cloned.1.call-done = bf16[192,192,128]{2,1,0:T(8,128)(2,1)} async-done(((bf16[12,192,128]{2,1,0:T(8,128)(2,1)}), bf16[192,192,128]{2,1,0:T(8,128)(2,1)}) %all-gather.11.cloned.1.call-update) | async-done | bytes 9437200 | tf_op jit(solution)/shard_map/all_gather | solution.py:114
  715.6 17.4 %copy.55 = bf16[192,192,128]{1,0,2:T(8,128)(2,1)} copy(bf16[192,192,128]{2,1,0:T(8,128)(2,1)} %all-gather.11.cloned.1.call-done) | data formatting | bytes 18874368 | tf_op jit(solution)/shard_map/all_gather | solution.py:114
  733.0 9.5 %fusion.84 = f32[128,192,12]{1,2,0:T(8,128)} fusion(bf16[192,192,128]{1,0,2:T(8,128)(2,1)} %copy.55, bf16[12,192,128]{1,0,2:T(8,128)(2,1)} %copy.59), kind=kOutput, calls=%fused_computation.145 | convolution fusion | flops 113246208 | bytes 11206656 | tf_op jit(solution)/shard_map/kjc,ijc->kic/dot_general | solution.py:117
  742.5 2.7 copy.60
  745.2 7.9 fusion.83
  753.1 2.7 copy.57
  755.8 3.7 bitcast_multiply_fusion.3
  759.5 1.2 fusion.47
  761.8 1.0 fusion.52
  762.9 1.1 fusion.55
  764.0 0.8 fusion.20
  764.8 1.7 fusion.18
  767.0 1.0 reshape.190
  768.0 2.5 fusion.22
  770.5 139.7 %all-gather.13.cloned.1.call-done = bf16[16,1,98560]{2,1,0:T(2,128)(2,1)} async-done(((bf16[1,1,98560]{2,1,0:T(2,128)(2,1)}), bf16[16,1,98560]{2,1,0:T(2,128)(2,1)}) %all-gather.13.cloned.1.call-update) | async-done | bytes 3153936 | tf_op jit(solution)/shard_map/all_gather | solution.py:11
  910.2 17.4 %reduce_sum.176 = bf16[98560]{0:T(1024)(128)(2,1)S(1)} reduce(bf16[16,1,98560]{2,1,0:T(2,128)(2,1)} %all-gather.13.cloned.1.call-done, bf16[]{:T(256)} %constant.38.clone.1), dimensions={0,1}, to_apply=%region_14.15 | reduce | flops 1478400 | bytes 3351042 | tf_op jit(solution)/shard_map/reduce_sum | solution.py:11
  (74 shorter events, 8.1 us)
Async XLA Ops:
  7.2 249.1 %copy-start = (bf16[128,512]{1,0:T(8,128)(2,1)S(1)}, bf16[128,512]{1,0:T(8,128)(2,1)}, u32[]{:S(2)}) copy-start(bf16[128,512]{1,0:T(8,128)(2,1)} %param.26) | copy-start | bytes 393220
  7.2 6.9 copy-start.5
  7.2 6.7 copy-start.15
  7.2 6.8 copy-start.17
  7.2 6.8 copy-start.10
  7.2 219.0 %all-gather.7.cloned.1.call-start = ((), (), s32[]{:S(2)}) async-start(), calls=%async_computation.1 | async-start | bytes 10027008 | tf_op jit(solution)/shard_map/all_gather | solution.py:74
  16.7 2.0 copy-start.18
  16.7 458.3 %all-gather.9.cloned.1.call-start = ((), (), s32[]{:S(2)}) async-start(), calls=%async_computation.2 | async-start | bytes 10027008 | tf_op jit(solution)/shard_map/all_gather | solution.py:96
  251.8 0.7 copy-start.16
  252.5 1.3 copy-start.8
  252.5 1.3 copy-start.11
  253.8 2.5 copy-start.14
  257.1 2.3 copy-start.1
  259.4 1.3 copy-start.6
  259.4 5.8 copy-start.12
  260.7 47.2 %all-to-all-start = ((bf16[12,192,128]{2,0,1:T(8,128)(2,1)}), bf16[12,192,128]{2,0,1:T(8,128)(2,1)}, u32[]{:S(2)}, u32[]{:S(2)}) async-start(bf16[12,192,128]{2,0,1:T(8,128)(2,1)} %copy.49), calls=%async_computation | async-start | bytes 1572864 | tf_op jit(solution)/shard_map/all_to_all | solution.py:91
  265.0 450.6 %all-gather.11.cloned.1.call-start = ((), (), s32[]{:S(2)}) async-start(), calls=%async_computation.3 | async-start | bytes 10027008 | tf_op jit(solution)/shard_map/all_gather | solution.py:114
  502.3 1.1 copy-start.2
  502.3 1.1 copy-start.9
  502.3 1.0 copy-start.13
  508.8 401.4 %all-gather.13.cloned.1.call-start = ((), (), s32[]{:S(2)}) async-start(), calls=%async_computation.4 | async-start | bytes 6702080 | tf_op jit(solution)/shard_map/all_gather | solution.py:11
  760.8 1.1 copy-start.7
  761.6 1.2 copy-start.3
  764.8 3.2 copy-start.4
Sparse Core Ops, SparseCore 0:
  16.8 209.3 all-gather.6
  259.5 215.4 all-gather.8
  508.9 206.6 all-gather.10
  768.1 142.0 all-gather.12
